TPU v7x, 256 devices: a whole 4x4x8 slice. The times are simulated.
256 devices in a mesh: dp: 8 (over z), expert: 32 (over x, y, core).
Axes of the slice: x: 4, y: 4, z: 8, core: 2. Of those that a mesh axis runs over, the one named last changes fastest.
Arguments:
- tokens: bfloat16 [65536, 2048], P(('dp', 'expert')), may hold values from -6 to 6
- expert_ranks: int32 [32, 65536], P(None, ('dp', 'expert')), may hold values from 0 to 65535, as said below
- capacity: int32 [32], replicated, may hold values from 512 to 1024, as said below
- weight_in: bfloat16 [32, 2048, 8192], P('expert', None, 'dp'), may hold values from -0.125 to 0.125
- weight_out: bfloat16 [32, 8192, 2048], P('expert', 'dp'), may hold values from -0.0625 to 0.0625
- gate_weights: float32 [32, 1024], P('expert', 'dp'), may hold values from 0.05 to 1
Outputs:
- combined: bfloat16 [65536, 2048], P(('dp', 'expert'))
Inputs may be any that keep to these rules, and one draw needn't show every extreme that they name: `expert_ranks`: for each expert the ranks are a permutation of 0 to 65535. Of the 256 tokens of one device, at most 8 have rank under 1024 for one expert; for an expert of capacity 1024, some devices have exactly 8. At least one expert has capacity 1024.
All inputs are finite; a program needn't handle non-finite values.
Results may differ from a plain program's by a relative error of at most 0.0053.
Values may be sent and summed in bfloat16 or wider, within the bound.
No kernel may reach another device: no remote copies, remote signals or barrier semaphores. Data moves between devices by JAX's collectives and lax.ppermute only.
A program may use at most 64 MiB of HBM per device.

v0:
```python
import jax
import jax.numpy as jnp
from jax import lax
from jax.sharding import Mesh
from jax.sharding import PartitionSpec as P

MOST = 8
EXPERT = ("expert_0", "expert_1", "expert_2")
DP_EXPERT = ("dp", "expert_0", "expert_1", "expert_2")


def exclusive(values):
    return jnp.cumsum(values) - values


def on_device(tokens, expert_ranks, capacity, weight_in, weight_out, gate_weights):
    dp_count = lax.axis_size("dp")
    expert_count = lax.axis_size(EXPERT)
    token_count, width = tokens.shape
    slots_dp = gate_weights.shape[1]
    rows_all = expert_count * MOST
    own_dp = lax.axis_index("dp")
    own_expert = lax.axis_index(EXPERT)
    chosen = expert_ranks < capacity[:, None]
    chosen_int = chosen.astype(jnp.int32)
    counts = jnp.sum(chosen_int, axis=1)
    before = jnp.cumsum(chosen_int, axis=1) - chosen_int
    places = lax.broadcasted_iota(jnp.int32, (expert_count, MOST, token_count), 1)
    pack_table = jnp.logical_and(chosen[:, None, :], before[:, None, :] == places)
    pack_table = pack_table.astype(jnp.bfloat16).reshape(rows_all, token_count)
    packed = jnp.dot(pack_table, tokens, preferred_element_type=jnp.float32).astype(jnp.bfloat16)
    arrived_rows = lax.all_to_all(
        packed.reshape(expert_count, MOST, width), EXPERT, split_axis=0, concat_axis=0, tiled=True
    ).reshape(rows_all, width)
    device_ids = lax.broadcasted_iota(jnp.int32, (expert_count, expert_count), 0)
    expert_ids = lax.broadcasted_iota(jnp.int32, (expert_count, expert_count), 1)
    table = lax.psum(jnp.where(device_ids == own_expert, counts[None, :], 0), EXPERT)
    plane_ids = lax.broadcasted_iota(jnp.int32, (dp_count, expert_count), 0)
    plane_counts = lax.psum(
        jnp.where(plane_ids == own_dp, jnp.sum(table, axis=0)[None, :], 0), "dp"
    )
    most_rows = jnp.max(plane_counts)
    arrived = jnp.sum(jnp.where(expert_ids == own_expert, table, 0), axis=1)
    earlier = jnp.logical_and(plane_ids < own_dp, expert_ids[:dp_count] == own_expert)
    first_slot = jnp.sum(jnp.where(earlier, plane_counts, 0))
    within = lax.broadcasted_iota(jnp.int32, (expert_count, MOST), 1)
    target = jnp.where(within < arrived[:, None], exclusive(arrived)[:, None] + within, -1).reshape(
        rows_all
    )
    gates_all = lax.all_gather(gate_weights[0], "dp", axis=0, tiled=True)
    gates_all = jnp.concatenate([gates_all, jnp.zeros((rows_all,), gates_all.dtype)])

    def experts(rows, plane_rows):
        slot_ids = lax.broadcasted_iota(jnp.int32, (rows_all, plane_rows), 1)
        place_table = (target[:, None] == slot_ids).astype(jnp.bfloat16)
        plane = lax.dot_general(
            place_table, rows, (((0,), (0,)), ((), ())), preferred_element_type=jnp.float32
        ).astype(jnp.bfloat16)
        slot_rows = lax.all_gather(plane, "dp", axis=0, tiled=True)
        hidden = jnp.maximum(
            jnp.dot(slot_rows, weight_in[0], preferred_element_type=jnp.float32), 0.0
        ).astype(jnp.bfloat16)
        share = jnp.dot(hidden, weight_out[0], preferred_element_type=jnp.float32)
        out = lax.psum_scatter(
            share.astype(jnp.bfloat16), "dp", scatter_dimension=0, tiled=True
        ).astype(jnp.float32)
        gates = lax.dynamic_slice_in_dim(gates_all, first_slot, plane_rows, 0)
        scaled = (gates[:, None] * out).astype(jnp.bfloat16)
        returned = jnp.dot(place_table, scaled, preferred_element_type=jnp.float32)
        return returned.astype(jnp.bfloat16)

    fair = slots_dp + slots_dp // 4
    sent_back = lax.cond(
        most_rows <= fair,
        lambda rows: experts(rows, fair),
        lambda rows: experts(rows, rows_all),
        arrived_rows,
    )
    results = lax.all_to_all(
        sent_back.reshape(expert_count, MOST, width),
        EXPERT,
        split_axis=0,
        concat_axis=0,
        tiled=True,
    ).reshape(rows_all, width)
    combined = lax.dot_general(
        pack_table, results, (((0,), (0,)), ((), ())), preferred_element_type=jnp.float32
    )
    return combined.astype(jnp.bfloat16)


def solution(mesh):
    split = Mesh(
        mesh.devices.reshape(mesh.shape["dp"], 4, 4, 2), ("dp", "expert_0", "expert_1", "expert_2")
    )
    placed = (
        P(DP_EXPERT, None),
        P(None, DP_EXPERT),
        P(),
        P(EXPERT, None, "dp"),
        P(EXPERT, "dp", None),
        P(EXPERT, "dp"),
    )
    return jax.shard_map(
        on_device, mesh=split, in_specs=placed, out_specs=P(DP_EXPERT, None), check_vma=False
    )
```

profile of v0, /device:TPU:1, one launch (start us, length us, event | category | flops | bytes accessed | tf_op | source)
XLA Modules:
  0.0 359.8 jit_solution(15286796204240877624)
XLA Ops:
  6.5 0.0 copy-start
  6.5 0.0 copy-start.1
  6.5 0.9 convert_bitcast_fusion.1
  7.5 0.6 reduce-window.11
  8.1 0.2 slice_reduce_fusion
  8.3 0.1 iota.68
  8.4 0.1 convert_subtract_fusion
  8.5 0.0 copy-done
  8.5 1.5 fusion.21
  10.0 8.6 %all-to-all-start = ((bf16[32,8,2048]{2,1,0:T(8,128)(2,1)}), bf16[32,8,2048]{2,1,0:T(8,128)(2,1)S(1)}, u32[]{:S(2)}, u32[]{:S(2)}) async-start(bf16[32,8,2048]{2,1,0:T(8,128)(2,1)} %fusion.21), calls=%async_computation.2 | async-start | bytes 2097152 | tf_op jit(solution)/shard_map/all_to_all | solution.py:32
  18.6 0.1 broadcast_select_fusion
  18.7 127.2 %psum.14 = s32[32,32]{1,0:T(8,128)S(1)} all-reduce(s32[32,32]{1,0:T(8,128)S(1)} %broadcast_select_fusion), channel_id=1, replica_groups=mesh['dp'=8,'expert_0'=4,'expert_1'=4,'expert_2'=2] {'expert_0','expert_..., use_global_device_ids=true, to_apply=%region_3.4 | all-reduce | flops 1024 | bytes 8192 | tf_op jit(solution)/shard_map/psum | solution.py:37
  145.9 0.1 select_reduce_fusion.2
  146.0 0.1 broadcast_select_fusion.1
  146.1 13.5 %psum.15 = s32[8,32]{1,0:T(8,128)S(1)} all-reduce(s32[8,32]{1,0:T(8,128)S(1)} %broadcast_select_fusion.1), channel_id=1, replica_groups=mesh['dp'=8,'expert_0'=4,'expert_1'=4,'expert_2'=2] {'dp'}, use_global_device_ids=true, to_apply=%region_5.6 | all-reduce | flops 256 | bytes 2048 | tf_op jit(solution)/shard_map/psum | solution.py:39
  159.6 0.7 reduce_max.9
  161.0 0.1 copy.25
  161.1 0.1 reduce-window.18
  161.2 0.0 copy-done.1
  161.2 10.9 %all-gather = f32[1,1024]{1,0:T(1,128)S(1)} all-gather(f32[1,128]{1,0:T(1,128)S(1)} %copy-done.1), channel_id=2, replica_groups=mesh['dp'=8,'expert_0'=4,'expert_1'=4,'expert_2'=2] {'dp'}, dimensions={1}, use_global_device_ids=true | all-gather | bytes 4608 | tf_op jit(solution)/shard_map/all_gather | solution.py:50
  172.0 0.0 all-to-all-done
  172.1 155.2 %conditional.2 = (bf16[256,2048]{1,0:T(8,128)(2,1)S(1)}) conditional(s32[]{:T(128)} %convert_element_type.51, (s32[32]{0:T(128)S(1)}, s32[32,8]{1,0:T(8,128)S(1)}, s32[32,1]{1,0:T(8,128)S(1)}, s32[32,8]{1,0:T(8,128)S(1)}, f32[1024]{0:T(1024)S(1)}, /*index=5*/s32[]{:T(128)}, s32[8]{0:T(128)S(1)}, pred[32]{0:T(512)(128)(4,1)S(1)}, ...), branch_computations={%region_9.12_spmd, %region_12.15_spmd} | conditional | flops 17727356928 | bytes 85999704
  172.1 0.0 all-gather.6.cloned.1.call-start
  172.1 0.1 copy.27
  172.2 0.1 add_select_fusion.1
  172.3 0.1 eq.45
  172.4 1.3 convolution_convert_fusion.3
  173.7 0.0 all-gather.6.cloned.1.call-update
  173.7 0.2 reduce-scatter.5.cloned.1.call-start
  174.0 70.5 %all-gather.6.cloned.1.call-done = bf16[1280,2048]{1,0:T(8,128)(2,1)} async-done(((bf16[160,2048]{1,0:T(8,128)(2,1)}), bf16[1280,2048]{1,0:T(8,128)(2,1)}) %all-gather.6.cloned.1.call-update) | async-done | bytes 5242896 | tf_op jit(solution)/shard_map/cond/branch_1_fun/all_gather | solution.py:59
  244.4 16.9 %convolution_convert_fusion.2 = bf16[1280,2048]{1,0:T(8,128)(2,1)} fusion(bf16[1,1024,2048]{2,1,0:T(8,128)(2,1)} %get-tuple-element.129, bf16[1280,2048]{1,0:T(8,128)(2,1)} %all-gather.6.cloned.1.call-done, bf16[1,2048,1024]{2,1,0:T(8,128)(2,1)} %get-tuple-element.128), kind=kOutput, calls=%fused_computation.19 | convolution fusion | flops 10742661120 | bytes 18874368 | tf_op jit(solution)/shard_map/cond/branch_1_fun/dot_general | solution.py:63
  261.3 0.0 reduce-scatter.5.cloned.1.call-update
  261.4 0.7 select_reduce_fusion.1
  264.0 0.1 pad_dynamic-slice_fusion.1
  264.1 61.4 %reduce-scatter.5.cloned.1.call-done = bf16[160,2048]{1,0:T(8,128)(2,1)} async-done(((bf16[1280,2048]{1,0:T(8,128)(2,1)}), bf16[160,2048]{1,0:T(8,128)(2,1)}) %reduce-scatter.5.cloned.1.call-update) | async-done | bytes 655376 | tf_op jit(solution)/shard_map/cond/branch_1_fun/reduce_scatter | solution.py:64
  325.4 1.6 fusion.15
  327.3 24.3 %all_to_all.10 = bf16[32,8,2048]{2,1,0:T(8,128)(2,1)S(1)} all-to-all(bf16[32,8,2048]{2,1,0:T(8,128)(2,1)S(1)} %bitcast.60), channel_id=1, replica_groups=mesh['dp'=8,'expert_0'=4,'expert_1'=4,'expert_2'=2] {'expert_0','expert_..., dimensions={0} | all-to-all | bytes 2097152 | tf_op jit(solution)/shard_map/all_to_all | solution.py:79
  351.5 1.5 fusion.20
  (11 shorter events, 0.1 us)
Async XLA Ops:
  6.5 2.0 copy-start
  6.5 154.6 %copy-start.1 = (f32[1,128]{1,0:T(1,128)S(1)}, f32[1,128]{1,0:T(1,128)}, u32[]{:S(2)}) copy-start(f32[1,128]{1,0:T(1,128)} %param.13) | copy-start | bytes 1540
  10.0 162.1 %all-to-all-start = ((bf16[32,8,2048]{2,1,0:T(8,128)(2,1)}), bf16[32,8,2048]{2,1,0:T(8,128)(2,1)S(1)}, u32[]{:S(2)}, u32[]{:S(2)}) async-start(bf16[32,8,2048]{2,1,0:T(8,128)(2,1)} %fusion.21), calls=%async_computation.2 | async-start | bytes 2097152 | tf_op jit(solution)/shard_map/all_to_all | solution.py:32
  172.1 72.3 %all-gather.6.cloned.1.call-start = ((), (), s32[]{:S(2)}) async-start(), calls=%async_computation.6 | async-start | bytes 5898240 | tf_op jit(solution)/shard_map/cond/branch_1_fun/all_gather | solution.py:59
  173.7 151.7 %reduce-scatter.5.cloned.1.call-start = ((), (), s32[]{:S(2)}) async-start(), calls=%async_computation.7 | async-start | bytes 5898240 | tf_op jit(solution)/shard_map/cond/branch_1_fun/reduce_scatter | solution.py:64
Sparse Core Ops, SparseCore 0:
  174.7 69.7 all-gather.5
  261.5 63.9 reduce-scatter.4
where the time goes:
time: 360 us
  blocking collectives  176 us (49%)
  waiting for transfers between devices  132 us (37%)
  matrix products  22.7 us (6%)
  between operations  14.1 us (4%)
  starting transfers between devices  8.84 us (2%)
    psum x1, blocking collectives, on_device(): lax.psum(jnp.where(device_ids == own_expert, counts[None, :], 0), EXPERT)  127 us
    all_gather x1, waiting for transfers between devices, experts(): slot_rows = lax.all_gather(plane, 'dp', axis=0, tiled=True)  70.5 us
    reduce_scatter x1, waiting for transfers between devices, experts(): lax.psum_scatter(share.astype(jnp.bfloat16), 'dp', scatter_dimension=0, t...  61.4 us
    all_to_all x1, blocking collectives, on_device(): lax.all_to_all(sent_back.reshape(expert_count, MOST, width), EXPERT, spli...  24.3 us
    dot_general x1, matrix products, experts(): share = jnp.dot(hidden, weight_out[0], preferred_element_type=jnp.float32)  16.9 us
    psum x1, blocking collectives, on_device(): lax.psum(jnp.where(plane_ids == own_dp, jnp.sum(table, axis=0)[None, :],...  13.5 us
    all_gather x1, blocking collectives, on_device(): gates_all = lax.all_gather(gate_weights[0], 'dp', axis=0, tiled=True)  10.9 us
    all_to_all x1, starting transfers between devices, on_device(): lax.all_to_all(packed.reshape(expert_count, MOST, width), EXPERT, split_a...  8.58 us
  transfers between devices with their start and end apart: 3, of which 2 were waited for; matrix products, arithmetic and copies ran while one was open for 1% of the time, Pallas kernels for 0%

commit v1 on v0

--- a/solution.py
+++ b/solution.py
@@ -34,7 +34,10 @@
     ).reshape(rows_all, width)
     device_ids = lax.broadcasted_iota(jnp.int32, (expert_count, expert_count), 0)
     expert_ids = lax.broadcasted_iota(jnp.int32, (expert_count, expert_count), 1)
-    table = lax.psum(jnp.where(device_ids == own_expert, counts[None, :], 0), EXPERT)
+    table = lax.psum(
+        lax.psum(jnp.where(device_ids == own_expert, counts[None, :], 0), ("expert_1", "expert_2")),
+        "expert_0",
+    )
     plane_ids = lax.broadcasted_iota(jnp.int32, (dp_count, expert_count), 0)
     plane_counts = lax.psum(
         jnp.where(plane_ids == own_dp, jnp.sum(table, axis=0)[None, :], 0), "dp"

time: 360 us -> 276 us (0.77)
  blocking collectives: 176 us -> 90.4 us
    psum x1 -> x2, blocking collectives: 127 us -> 41.7 us  [the longest x1 25.1 us: on_device(): lax.psum(jnp.where(device_ids == own_expert, counts[None, :], 0), ('exper...]
where the time goes in v1:
time: 276 us
  waiting for transfers between devices  133 us (48%)
  blocking collectives  90.4 us (33%)
  matrix products  22.7 us (8%)
  between operations  14.1 us (5%)
  starting transfers between devices  8.84 us (3%)
  other arithmetic  3.51 us (1%)
    all_gather x1, waiting for transfers between devices, experts(): slot_rows = lax.all_gather(plane, 'dp', axis=0, tiled=True)  71.9 us
    reduce_scatter x1, waiting for transfers between devices, experts(): lax.psum_scatter(share.astype(jnp.bfloat16), 'dp', scatter_dimension=0, t...  61.3 us
    psum x1, blocking collectives, on_device(): lax.psum(jnp.where(device_ids == own_expert, counts[None, :], 0), ('exper...  25.1 us
    all_to_all x1, blocking collectives, on_device(): lax.all_to_all(sent_back.reshape(expert_count, MOST, width), EXPERT, spli...  24.3 us
    dot_general x1, matrix products, experts(): share = jnp.dot(hidden, weight_out[0], preferred_element_type=jnp.float32)  16.9 us
    psum x1, blocking collectives, on_device(): lax.psum(lax.psum(jnp.where(device_ids == own_expert, counts[None, :], 0)...  16.7 us
    psum x1, blocking collectives, on_device(): lax.psum(jnp.where(plane_ids == own_dp, jnp.sum(table, axis=0)[None, :],...  13.2 us
    all_gather x1, blocking collectives, on_device(): gates_all = lax.all_gather(gate_weights[0], 'dp', axis=0, tiled=True)  11.1 us
  transfers between devices with their start and end apart: 3, of which 2 were waited for; matrix products, arithmetic and copies ran while one was open for 1% of the time, Pallas kernels for 0%

profile of v1, /device:TPU:1, one launch (start us, length us, event | category | flops | bytes accessed | tf_op | source)
XLA Modules:
  0.0 275.8 jit_solution(6664103881473524336)
XLA Ops:
  6.5 0.0 copy-start
  6.5 0.0 copy-start.1
  6.5 0.9 convert_bitcast_fusion.1
  7.5 0.6 reduce-window.11
  8.1 0.2 slice_reduce_fusion
  8.3 0.1 iota.68
  8.4 0.1 convert_subtract_fusion
  8.5 0.0 copy-done
  8.5 1.5 fusion.21
  10.0 8.6 %all-to-all-start = ((bf16[32,8,2048]{2,1,0:T(8,128)(2,1)}), bf16[32,8,2048]{2,1,0:T(8,128)(2,1)S(1)}, u32[]{:S(2)}, u32[]{:S(2)}) async-start(bf16[32,8,2048]{2,1,0:T(8,128)(2,1)} %fusion.21), calls=%async_computation.2 | async-start | bytes 2097152 | tf_op jit(solution)/shard_map/all_to_all | solution.py:32
  18.6 0.1 broadcast_select_fusion
  18.7 25.1 %psum.21 = s32[32,32]{1,0:T(8,128)S(1)} all-reduce(s32[32,32]{1,0:T(8,128)S(1)} %broadcast_select_fusion), channel_id=1, replica_groups=mesh['dp'=8,'expert_0'=4,'expert_1'=4,'expert_2'=2] {'expert_1','expert_2'}, use_global_device_ids=true, to_apply=%region_3.4 | all-reduce | flops 1024 | bytes 8192 | tf_op jit(solution)/shard_map/psum | solution.py:38
  43.7 16.7 %psum.22 = s32[32,32]{1,0:T(8,128)S(1)} all-reduce(s32[32,32]{1,0:T(8,128)S(1)} %psum.21), channel_id=1, replica_groups=mesh['dp'=8,'expert_0'=4,'expert_1'=4,'expert_2'=2] {'expert_0'}, use_global_device_ids=true, to_apply=%region_4.5 | all-reduce | flops 1024 | bytes 8192 | tf_op jit(solution)/shard_map/psum | solution.py:37
  60.4 0.1 select_reduce_fusion.2
  60.5 0.1 broadcast_select_fusion.1
  60.6 13.2 %psum.23 = s32[8,32]{1,0:T(8,128)S(1)} all-reduce(s32[8,32]{1,0:T(8,128)S(1)} %broadcast_select_fusion.1), channel_id=1, replica_groups=mesh['dp'=8,'expert_0'=4,'expert_1'=4,'expert_2'=2] {'dp'}, use_global_device_ids=true, to_apply=%region_6.7 | all-reduce | flops 256 | bytes 2048 | tf_op jit(solution)/shard_map/psum | solution.py:42
  73.8 0.7 reduce_max.9
  75.2 0.1 copy.25
  75.3 0.1 reduce-window.18
  75.4 0.0 copy-done.1
  75.4 11.1 %all-gather = f32[1,1024]{1,0:T(1,128)S(1)} all-gather(f32[1,128]{1,0:T(1,128)S(1)} %copy-done.1), channel_id=2, replica_groups=mesh['dp'=8,'expert_0'=4,'expert_1'=4,'expert_2'=2] {'dp'}, dimensions={1}, use_global_device_ids=true | all-gather | bytes 4608 | tf_op jit(solution)/shard_map/all_gather | solution.py:53
  86.5 0.0 all-to-all-done
  86.6 156.6 %conditional.2 = (bf16[256,2048]{1,0:T(8,128)(2,1)S(1)}) conditional(s32[]{:T(128)} %convert_element_type.51, (s32[32]{0:T(128)S(1)}, s32[32,8]{1,0:T(8,128)S(1)}, s32[32,1]{1,0:T(8,128)S(1)}, s32[32,8]{1,0:T(8,128)S(1)}, f32[1024]{0:T(1024)S(1)}, /*index=5*/s32[]{:T(128)}, s32[8]{0:T(128)S(1)}, pred[32]{0:T(512)(128)(4,1)S(1)}, ...), branch_computations={%region_10.13_spmd, %region_13.16_spmd} | conditional | flops 17727356928 | bytes 85999704
  86.6 0.0 all-gather.6.cloned.1.call-start
  86.6 0.1 copy.27
  86.7 0.1 add_select_fusion.1
  86.8 0.1 eq.45
  86.9 1.3 convolution_convert_fusion.3
  88.2 0.0 all-gather.6.cloned.1.call-update
  88.2 0.2 reduce-scatter.5.cloned.1.call-start
  88.4 71.9 %all-gather.6.cloned.1.call-done = bf16[1280,2048]{1,0:T(8,128)(2,1)} async-done(((bf16[160,2048]{1,0:T(8,128)(2,1)}), bf16[1280,2048]{1,0:T(8,128)(2,1)}) %all-gather.6.cloned.1.call-update) | async-done | bytes 5242896 | tf_op jit(solution)/shard_map/cond/branch_1_fun/all_gather | solution.py:62
  160.4 16.9 %convolution_convert_fusion.2 = bf16[1280,2048]{1,0:T(8,128)(2,1)} fusion(bf16[1,1024,2048]{2,1,0:T(8,128)(2,1)} %get-tuple-element.129, bf16[1280,2048]{1,0:T(8,128)(2,1)} %all-gather.6.cloned.1.call-done, bf16[1,2048,1024]{2,1,0:T(8,128)(2,1)} %get-tuple-element.128), kind=kOutput, calls=%fused_computation.19 | convolution fusion | flops 10742661120 | bytes 18874368 | tf_op jit(solution)/shard_map/cond/branch_1_fun/dot_general | solution.py:66
  177.3 0.0 reduce-scatter.5.cloned.1.call-update
  177.3 0.7 select_reduce_fusion.1
  179.9 0.1 pad_dynamic-slice_fusion.1
  180.0 61.3 %reduce-scatter.5.cloned.1.call-done = bf16[160,2048]{1,0:T(8,128)(2,1)} async-done(((bf16[1280,2048]{1,0:T(8,128)(2,1)}), bf16[160,2048]{1,0:T(8,128)(2,1)}) %reduce-scatter.5.cloned.1.call-update) | async-done | bytes 655376 | tf_op jit(solution)/shard_map/cond/branch_1_fun/reduce_scatter | solution.py:67
  241.4 1.6 fusion.15
  243.2 24.3 %all_to_all.10 = bf16[32,8,2048]{2,1,0:T(8,128)(2,1)S(1)} all-to-all(bf16[32,8,2048]{2,1,0:T(8,128)(2,1)S(1)} %bitcast.60), channel_id=1, replica_groups=mesh['dp'=8,'expert_0'=4,'expert_1'=4,'expert_2'=2] {'expert_0','expert_..., dimensions={0} | all-to-all | bytes 2097152 | tf_op jit(solution)/shard_map/all_to_all | solution.py:82
  267.5 1.5 fusion.20
  (11 shorter events, 0.1 us)
Async XLA Ops:
  6.5 2.0 copy-start
  6.5 68.9 %copy-start.1 = (f32[1,128]{1,0:T(1,128)S(1)}, f32[1,128]{1,0:T(1,128)}, u32[]{:S(2)}) copy-start(f32[1,128]{1,0:T(1,128)} %param.13) | copy-start | bytes 1540
  10.0 76.6 %all-to-all-start = ((bf16[32,8,2048]{2,1,0:T(8,128)(2,1)}), bf16[32,8,2048]{2,1,0:T(8,128)(2,1)S(1)}, u32[]{:S(2)}, u32[]{:S(2)}) async-start(bf16[32,8,2048]{2,1,0:T(8,128)(2,1)} %fusion.21), calls=%async_computation.2 | async-start | bytes 2097152 | tf_op jit(solution)/shard_map/all_to_all | solution.py:32
  86.6 73.8 %all-gather.6.cloned.1.call-start = ((), (), s32[]{:S(2)}) async-start(), calls=%async_computation.6 | async-start | bytes 5898240 | tf_op jit(solution)/shard_map/cond/branch_1_fun/all_gather | solution.py:62
  88.2 153.2 %reduce-scatter.5.cloned.1.call-start = ((), (), s32[]{:S(2)}) async-start(), calls=%async_computation.7 | async-start | bytes 5898240 | tf_op jit(solution)/shard_map/cond/branch_1_fun/reduce_scatter | solution.py:67
Sparse Core Ops, SparseCore 0:
  89.2 71.1 all-gather.5
  177.4 63.9 reduce-scatter.4
